TPU v7x, 256 devices: a whole 4x4x8 slice. The times are simulated.
256 devices in a mesh: fy: 8 (over x, core), fx: 16 (over y, z_lo), ch: 2 (over z_hi).
Axes of the slice: x: 4, y: 4, z: 8 (z_hi: 2, z_lo: 4; z = z_hi * 4 + z_lo), core: 2. Of those that a mesh axis runs over, the one named last changes fastest.
Arguments:
- image_cube: float32 [64, 1024, 1664], P('ch', 'fx', 'fy'), may hold values from 0 to 2
- data_grad: bfloat16 [64, 1024, 1664], P('ch', 'fx', 'fy'), may hold values from -6 to 6
- dual_coeffs: float32 [64, 1792, 2048], P('ch', 'fx', 'fy'), may hold values from -6 to 6
- reweights: float32 [1792, 2048], P('fx', 'fy'), may hold values from 1 to 40
Outputs:
- image_next: float32 [64, 1024, 1664], P('ch', 'fx', 'fy')
- dual_next: float32 [64, 1792, 2048], P('ch', 'fx', 'fy')
All inputs are finite; a program needn't handle non-finite values.
Results may differ from a plain program's by a relative error of at most 0.0003.
Values sent between devices are 32-bit elements; how exact they have to be, the bound alone decides.
A program may use at most 64 MiB of HBM per device.

v0:
```python
import jax
import jax.numpy as jnp
import numpy as np
from jax import lax
from jax.sharding import PartitionSpec as P

LEVELS = 2


LOW_PASS = [
    -0.00011747678400228192,
    0.0006754494059985568,
    -0.0003917403729959771,
    -0.00487035299301066,
    0.008746094047015655,
    0.013981027917015516,
    -0.04408825393106472,
    -0.01736930100202211,
    0.128747426620186,
    0.00047248457399797254,
    -0.2840155429624281,
    -0.015829105256023893,
    0.5853546836548691,
    0.6756307362980128,
    0.3128715909144659,
    0.05441584224308161,
]
TAU_STEP = 0.5
LAMBDA_REG = 1.0
EPSILON = 1e-06


def passed_along(array, axis, by):
    length = lax.axis_size(axis)
    pairs = [(i, i + by) for i in range(length) if 0 <= i + by < length]
    return lax.ppermute(array, axis, pairs)


def total_of_pieces(array, axis):
    return lax.all_gather(array, axis).sum(0)


def level_matrix(length):
    halved = length // 2
    taps_count = len(LOW_PASS)
    matrix = np.zeros((length, length))
    for out_row in range(halved):
        for tap_index in range(taps_count):
            column = (2 * out_row + tap_index) % length
            matrix[out_row, column] += LOW_PASS[tap_index]
            matrix[halved + out_row, column] += (-1) ** tap_index * LOW_PASS[
                taps_count - 1 - tap_index
            ]
    return matrix


def analysis(facet_block, levels):
    result = facet_block
    width_x = facet_block.shape[1]
    width_y = facet_block.shape[2]
    for level_step in range(levels):
        matrix_x = jnp.asarray(level_matrix(width_x), dtype=jnp.float32)
        matrix_y = jnp.asarray(level_matrix(width_y), dtype=jnp.float32)
        corner_part = result[:, :width_x, :width_y]
        corner_part = jnp.einsum(
            "cxy,vy->cxv", corner_part, matrix_y, precision=lax.Precision.HIGHEST
        )
        corner_part = jnp.einsum(
            "ux,cxv->cuv", matrix_x, corner_part, precision=lax.Precision.HIGHEST
        )
        result = result.at[:, :width_x, :width_y].set(corner_part)
        width_x = width_x // 2
        width_y = width_y // 2
    return result


def synthesis(coeff_block, levels):
    result = coeff_block
    for level_step in range(levels - 1, -1, -1):
        width_x = coeff_block.shape[1] // 2**level_step
        width_y = coeff_block.shape[2] // 2**level_step
        matrix_x = jnp.asarray(level_matrix(width_x), dtype=jnp.float32)
        matrix_y = jnp.asarray(level_matrix(width_y), dtype=jnp.float32)
        corner_part = result[:, :width_x, :width_y]
        corner_part = jnp.einsum(
            "ux,cuv->cxv", matrix_x, corner_part, precision=lax.Precision.HIGHEST
        )
        corner_part = jnp.einsum(
            "cxv,vy->cxy", corner_part, matrix_y, precision=lax.Precision.HIGHEST
        )
        result = result.at[:, :width_x, :width_y].set(corner_part)
    return result


def tile_weights(length, intersection, position_index, count):
    positions = jnp.arange(length, dtype=jnp.int32)
    edge = (positions >= length - intersection) & (position_index < count - 1)
    return jnp.where(edge, 0.5**0.5, 1.0).astype(jnp.float32)


def add_tail(base, tail, along):
    length = base.shape[along]
    keep = length - tail.shape[along]
    head = lax.slice_in_dim(base, 0, keep, axis=along)
    rest = lax.slice_in_dim(base, keep, length, axis=along)
    return jnp.concatenate([head, rest + tail], axis=along)


def shards(image_cube, data_grad, dual_coeffs, reweights):
    tile_x = image_cube.shape[1]
    tile_y = image_cube.shape[2]
    intersection = dual_coeffs.shape[1] - tile_x
    weight_map = (
        tile_weights(tile_x, intersection, lax.axis_index("fx"), lax.axis_size("fx"))[:, None]
        * tile_weights(tile_y, intersection, lax.axis_index("fy"), lax.axis_size("fy"))[None, :]
    )
    synthesized = synthesis(dual_coeffs, LEVELS)
    incoming = passed_along(synthesized[:, :intersection, :], "fx", -1)
    own_cols = add_tail(synthesized[:, intersection:, :], incoming, 1)
    incoming_rows = passed_along(own_cols[:, :, :intersection], "fy", -1)
    summed = add_tail(own_cols[:, :, intersection:], incoming_rows, 2)
    adjoint = summed * weight_map
    image_next = jnp.maximum(image_cube - TAU_STEP * (data_grad.astype(jnp.float32) + adjoint), 0.0)
    extrap = (2.0 * image_next - image_cube) * weight_map
    border = passed_along(extrap[:, tile_x - intersection :, :], "fx", 1)
    rows_block = jnp.concatenate([border, extrap], axis=1)
    border_rows = passed_along(rows_block[:, :, tile_y - intersection :], "fy", 1)
    extended = jnp.concatenate([border_rows, rows_block], axis=2)
    updated = dual_coeffs + analysis(extended, LEVELS)
    squared_sum = jnp.sum(updated * updated, axis=0)
    totals = total_of_pieces(squared_sum, "ch")
    factor = jnp.minimum(1.0, LAMBDA_REG * reweights / jnp.sqrt(totals + EPSILON))
    dual_next = updated * factor[None]
    return (image_next, dual_next)


def solution(mesh):
    return jax.shard_map(
        shards,
        mesh=mesh,
        in_specs=(P("ch", "fx", "fy"), P("ch", "fx", "fy"), P("ch", "fx", "fy"), P("fx", "fy")),
        out_specs=(P("ch", "fx", "fy"), P("ch", "fx", "fy")),
        check_vma=False,
    )
```

profile of v0, /device:TPU:22, one launch (start us, length us, event | category | flops | bytes accessed | tf_op | source)
XLA Modules:
  0.0 163.2 jit_solution(1847189346338398456)
XLA Ops:
  0.7 0.7 copy-done.11
  1.4 1.3 copy-done
  2.7 0.9 convolution_bitcast_fusion.2
  3.8 0.9 convolution_dynamic-update-slice_fusion
  4.7 3.6 %fusion.21 = f32[32,256,112]{1,2,0:T(8,128)S(1)} fusion(f32[32,112,256]{2,1,0:T(8,128)S(1)} %convolution_dynamic-update-slice_fusion, f32[112,112,1]{0,1,2:T(8,128)S(1)} %copy-done.9), kind=kOutput, calls=%fused_computation.39 | convolution fusion | flops 1233125376 | bytes 7390208 | tf_op jit(solution)/shard_map/ux,cuv->cxv/dot_general | solution.py:85
  8.4 3.2 %fusion.6 = f32[32,112,256]{2,1,0:T(8,128)S(1)} fusion(f32[256,256,1]{1,0,2:T(8,128)S(1)} %copy-done.7, f32[32,256,112]{1,2,0:T(8,128)S(1)} %fusion.21), kind=kOutput, calls=%fused_computation.6 | convolution fusion | flops 2818572288 | bytes 7602176 | tf_op jit(solution)/shard_map/cxv,vy->cxy/dot_general | solution.py:88
  11.7 6.4 %collective-permute-start = (f32[32,48,256]{2,1,0:T(8,128)S(1)}, f32[32,48,256]{2,1,0:T(8,128)}, u32[]{:S(2)}, u32[]{:S(2)}) collective-permute-start(f32[32,48,256]{2,1,0:T(8,128)S(1)} %slice.138), channel_id=1, source_target_pairs={{2,0},{4,2},{6,4},{8,6},{10,8},{12,10},{14,12},{16,14},{18,16},{20... | collective-permute-start | bytes 4718600 | tf_op jit(solution)/shard_map/ppermute | solution.py:36
  18.2 33.5 %collective-permute-done = f32[32,48,256]{2,1,0:T(8,128)} collective-permute-done((f32[32,48,256]{2,1,0:T(8,128)S(1)}, f32[32,48,256]{2,1,0:T(8,128)}, u32[]{:S(2)}, u32[]{:S(2)}) %collective-permute-start) | collective-permute-done | bytes 1572896 | tf_op jit(solution)/shard_map/ppermute | solution.py:36
  51.8 2.1 %slice_add_fusion = f32[32,48,256]{2,1,0:T(8,128)S(1)} fusion(f32[32,48,256]{2,1,0:T(8,128)} %collective-permute-done, f32[32,112,256]{2,1,0:T(8,128)} %copy-done.3), kind=kLoop, calls=%fused_computation.23 | loop fusion | flops 393216 | bytes 4718592 | tf_op jit(solution)/shard_map/add | solution.py:106
  54.0 1.2 copy.18
  55.2 1.9 %collective-permute-start.1 = (f32[32,64,48]{1,2,0:T(8,128)}, f32[32,64,48]{1,2,0:T(8,128)}, u32[]{:S(2)}, u32[]{:S(2)}) collective-permute-start(f32[32,64,48]{1,2,0:T(8,128)} %copy.18), channel_id=1, source_target_pairs={{32,0},{64,32},{96,64},{128,96},{160,128},{192,160},{224,192},{33,... | collective-permute-start | bytes 1179656 | tf_op jit(solution)/shard_map/ppermute | solution.py:36
  57.2 1.9 %fusion.8 = f32[32,64,160]{2,1,0:T(8,128)} fusion(f32[32,48,256]{2,1,0:T(8,128)S(1)} %slice_add_fusion, f32[32,16,256]{2,1,0:T(8,128)S(1)} %slice.136), kind=kLoop, calls=%fused_computation.13 | loop fusion | flops 327680 | bytes 3407872 | tf_op jit(solution)/shard_map/concatenate | solution.py:106
  59.1 7.8 %collective-permute-done.1 = f32[32,64,48]{1,2,0:T(8,128)} collective-permute-done((f32[32,64,48]{1,2,0:T(8,128)}, f32[32,64,48]{1,2,0:T(8,128)}, u32[]{:S(2)}, u32[]{:S(2)}) %collective-permute-start.1) | collective-permute-done | bytes 393248 | tf_op jit(solution)/shard_map/ppermute | solution.py:36
  66.9 1.5 copy.19
  68.7 1.2 copy-done.4
  70.0 0.6 copy-done.6
  70.6 3.4 %subtract_multiply_fusion = (f32[32,64,208]{2,1,0:T(8,128)S(1)}, f32[32,64,208]{2,1,0:T(8,128)}) fusion(f32[32,64,208]{2,1,0:T(8,128)S(1)} %copy-done.6, f32[64,208]{1,0:T(8,128)S(1)} %broadcast_multiply_fusion.1, f32[32,64,48]{2,1,0:T(8,128)S(1)} %fusion.15, f32[32,64,160]{2,1,0:T(8,128)S(1)} %copy-done.4, bf16[32,64,208]{2,1,0:T(8,128)(2,1)} %param.25), kind=kLoop, calls=%fused_computation.19 | loop fusion | flops 4259840 | bytes 7720960 | tf_op jit(solution)/shard_map/mul | solution.py:124
  74.1 2.3 %collective-permute-start.2 = (f32[32,48,208]{2,1,0:T(8,128)S(1)}, f32[32,48,208]{2,1,0:T(8,128)S(1)}, u32[]{:S(2)}, u32[]{:S(2)}) collective-permute-start(f32[32,48,208]{2,1,0:T(8,128)S(1)} %slice.143), channel_id=1, source_target_pairs={{0,2},{2,4},{4,6},{6,8},{8,10},{10,12},{12,14},{14,16},{16,18},{18... | collective-permute-start | bytes 3833864 | tf_op jit(solution)/shard_map/ppermute | solution.py:36
  76.4 33.1 %collective-permute-done.2 = f32[32,48,208]{2,1,0:T(8,128)S(1)} collective-permute-done((f32[32,48,208]{2,1,0:T(8,128)S(1)}, f32[32,48,208]{2,1,0:T(8,128)S(1)}, u32[]{:S(2)}, u32[]{:S(2)}) %collective-permute-start.2) | collective-permute-done | bytes 1277984 | tf_op jit(solution)/shard_map/ppermute | solution.py:36
  109.5 1.2 copy-done.5
  110.7 1.8 %pad_maximum_fusion = f32[32,112,48]{2,1,0:T(8,128)} fusion(f32[32,64,208]{2,1,0:T(8,128)S(1)} %get-tuple-element.68, f32[32,48,208]{2,1,0:T(8,128)S(1)} %collective-permute-done.2), kind=kLoop, calls=%fused_computation.21 | loop fusion | flops 172032 | bytes 3670016 | tf_op jit(solution)/shard_map/concatenate | solution.py:126
  112.4 2.0 %copy.20 = f32[32,112,48]{1,2,0:T(8,128)S(1)} copy(f32[32,112,48]{2,1,0:T(8,128)} %pad_maximum_fusion) | data formatting | bytes 1376256 | tf_op jit(solution)/shard_map/slice | solution.py:127
  114.4 1.9 %collective-permute-start.3 = (f32[32,112,48]{1,2,0:T(8,128)S(1)}, f32[32,112,48]{1,2,0:T(8,128)}, u32[]{:S(2)}, u32[]{:S(2)}) collective-permute-start(f32[32,112,48]{1,2,0:T(8,128)S(1)} %copy.20), channel_id=1, source_target_pairs={{0,32},{32,64},{64,96},{96,128},{128,160},{160,192},{192,224},{1,3... | collective-permute-start | bytes 2064392 | tf_op jit(solution)/shard_map/ppermute | solution.py:36
  116.4 17.1 %collective-permute-done.3 = f32[32,112,48]{1,2,0:T(8,128)} collective-permute-done((f32[32,112,48]{1,2,0:T(8,128)S(1)}, f32[32,112,48]{1,2,0:T(8,128)}, u32[]{:S(2)}, u32[]{:S(2)}) %collective-permute-start.3) | collective-permute-done | bytes 688160 | tf_op jit(solution)/shard_map/ppermute | solution.py:36
  133.5 2.9 %copy.21 = f32[32,112,48]{2,1,0:T(8,128)} copy(f32[32,112,48]{1,2,0:T(8,128)} %collective-permute-done.3) | data formatting | bytes 1376256 | tf_op jit(solution)/shard_map/ppermute | solution.py:36
  136.4 5.1 %fusion = f32[32,112,256]{2,1,0:T(8,128)S(1)} fusion(f32[256,256,1]{1,0,2:T(8,128)S(1)} %copy-done.7, f32[32,64,208]{2,1,0:T(8,128)S(1)} %get-tuple-element.68, f32[32,48,208]{2,1,0:T(8,128)} %copy-done.5, f32[32,112,48]{2,1,0:T(8,128)} %copy.21), kind=kOutput, calls=%fused_computation | convolution fusion | flops 2820407296 | bytes 7602176 | tf_op jit(solution)/shard_map/cxy,vy->cxv/dot_general | solution.py:65
  141.5 3.7 %convolution_bitcast_fusion = f32[32,112,256]{2,1,0:T(8,128)S(1)} fusion(f32[32,112,256]{2,1,0:T(8,128)S(1)} %fusion, f32[112,112,1]{0,1,2:T(8,128)S(1)} %copy-done.10), kind=kOutput, calls=%fused_computation.20 | convolution fusion | flops 1233125376 | bytes 7390208 | tf_op jit(solution)/shard_map/ux,cxv->cuv/dot_general | solution.py:68
  145.2 0.9 fusion.16
  146.1 0.9 fusion.13
  147.2 2.5 %multiply_reduce_fusion = (f32[112,256]{1,0:T(8,128)S(1)}, f32[32,112,256]{2,1,0:T(8,128)}) fusion(f32[32,112,256]{2,1,0:T(8,128)S(1)} %copy-done.1, f32[32,112,256]{2,1,0:T(8,128)S(1)} %fusion.13), kind=kLoop, calls=%fused_computation.8 | loop fusion | flops 2723840 | bytes 11124736 | tf_op jit(solution)/shard_map/reduce_sum | solution.py:130
  149.7 9.4 %all-gather = f32[224,256]{1,0:T(8,128)S(1)} all-gather(f32[112,256]{1,0:T(8,128)S(1)} %get-tuple-element.66), channel_id=2, replica_groups=mesh['fy'=8,'fx'=16,'ch'=2] {'ch'}, dimensions={0}, use_global_device_ids=true | all-gather | bytes 344064 | tf_op jit(solution)/shard_map/all_gather | solution.py:40
  159.1 4.1 %broadcast_multiply_fusion = f32[32,112,256]{2,1,0:T(8,128)} fusion(f32[32,112,256]{2,1,0:T(8,128)} %get-tuple-element.67, f32[112,256]{1,0:T(8,128)S(1)} %multiply_minimum_fusion), kind=kLoop, calls=%fused_computation.22 | loop fusion | flops 917504 | bytes 7454720 | tf_op jit(solution)/shard_map/mul | solution.py:133
  (33 shorter events, 1.3 us)
Async XLA Ops:
  0.6 0.8 copy-start.11
  0.6 3.0 %copy-start.8 = (f32[128,128,1]{1,0,2:T(8,128)S(1)}, f32[128,128,1]{1,0,2:T(8,128)}, u32[]{:S(2)}) copy-start(f32[128,128,1]{1,0,2:T(8,128)} %constant.164) | copy-start | bytes 196612
  0.7 2.1 %copy-start = (f32[32,112,256]{2,1,0:T(8,128)S(1)}, f32[32,112,256]{2,1,0:T(8,128)}, u32[]{:S(2)}) copy-start(f32[32,112,256]{2,1,0:T(8,128)} %param.26) | copy-start | bytes 11010052
  0.7 3.2 %copy-start.2 = (f32[32,112,256]{2,1,0:T(8,128)S(1)}, f32[32,112,256]{2,1,0:T(8,128)}, u32[]{:S(2)}) copy-start(f32[32,112,256]{2,1,0:T(8,128)} %param.26) | copy-start | bytes 11010052
  2.7 2.0 %copy-start.9 = (f32[112,112,1]{0,1,2:T(8,128)S(1)}, f32[112,112,1]{0,1,2:T(8,128)}, u32[]{:S(2)}) copy-start(f32[112,112,1]{0,1,2:T(8,128)} %constant.165) | copy-start | bytes 150532
  4.7 3.6 %copy-start.7 = (f32[256,256,1]{1,0,2:T(8,128)S(1)}, f32[256,256,1]{1,0,2:T(8,128)}, u32[]{:S(2)}) copy-start(f32[256,256,1]{1,0,2:T(8,128)} %constant.166) | copy-start | bytes 786436
  11.6 6.6 %copy-start.3 = (f32[32,112,256]{2,1,0:T(8,128)}, f32[32,112,256]{2,1,0:T(8,128)S(1)}, u32[]{:S(2)}) copy-start(f32[32,112,256]{2,1,0:T(8,128)S(1)} %fusion.6) | copy-start | bytes 11010052
  11.7 40.1 %collective-permute-start = (f32[32,48,256]{2,1,0:T(8,128)S(1)}, f32[32,48,256]{2,1,0:T(8,128)}, u32[]{:S(2)}, u32[]{:S(2)}) collective-permute-start(f32[32,48,256]{2,1,0:T(8,128)S(1)} %slice.138), channel_id=1, source_target_pairs={{2,0},{4,2},{6,4},{8,6},{10,8},{12,10},{14,12},{16,14},{18,16},{20... | collective-permute-start | bytes 4718600 | tf_op jit(solution)/shard_map/ppermute | solution.py:36
  55.2 11.7 %collective-permute-start.1 = (f32[32,64,48]{1,2,0:T(8,128)}, f32[32,64,48]{1,2,0:T(8,128)}, u32[]{:S(2)}, u32[]{:S(2)}) collective-permute-start(f32[32,64,48]{1,2,0:T(8,128)} %copy.18), channel_id=1, source_target_pairs={{32,0},{64,32},{96,64},{128,96},{160,128},{192,160},{224,192},{33,... | collective-permute-start | bytes 1179656 | tf_op jit(solution)/shard_map/ppermute | solution.py:36
  68.4 1.6 copy-start.4
  68.4 2.2 %copy-start.6 = (f32[32,64,208]{2,1,0:T(8,128)S(1)}, f32[32,64,208]{2,1,0:T(8,128)}, u32[]{:S(2)}) copy-start(f32[32,64,208]{2,1,0:T(8,128)} %param.24) | copy-start | bytes 5111812
  74.1 35.4 %collective-permute-start.2 = (f32[32,48,208]{2,1,0:T(8,128)S(1)}, f32[32,48,208]{2,1,0:T(8,128)S(1)}, u32[]{:S(2)}, u32[]{:S(2)}) collective-permute-start(f32[32,48,208]{2,1,0:T(8,128)S(1)} %slice.143), channel_id=1, source_target_pairs={{0,2},{2,4},{4,6},{6,8},{8,10},{10,12},{12,14},{14,16},{16,18},{18... | collective-permute-start | bytes 3833864 | tf_op jit(solution)/shard_map/ppermute | solution.py:36
  109.5 1.2 copy-start.5
  114.4 19.0 %collective-permute-start.3 = (f32[32,112,48]{1,2,0:T(8,128)S(1)}, f32[32,112,48]{1,2,0:T(8,128)}, u32[]{:S(2)}, u32[]{:S(2)}) collective-permute-start(f32[32,112,48]{1,2,0:T(8,128)S(1)} %copy.20), channel_id=1, source_target_pairs={{0,32},{32,64},{64,96},{96,128},{128,160},{160,192},{192,224},{1,3... | collective-permute-start | bytes 2064392 | tf_op jit(solution)/shard_map/ppermute | solution.py:36
  136.4 5.1 %copy-start.10 = (f32[112,112,1]{0,1,2:T(8,128)S(1)}, f32[112,112,1]{0,1,2:T(8,128)}, u32[]{:S(2)}) copy-start(f32[112,112,1]{0,1,2:T(8,128)} %constant.165) | copy-start | bytes 150532
  141.5 4.6 %copy-start.12 = (f32[56,56,1]{0,1,2:T(8,128)S(1)}, f32[56,56,1]{0,1,2:T(8,128)}, u32[]{:S(2)}) copy-start(f32[56,56,1]{0,1,2:T(8,128)} %constant.163) | copy-start | bytes 37636
  145.1 2.0 %copy-start.1 = (f32[32,112,256]{2,1,0:T(8,128)S(1)}, f32[32,112,256]{2,1,0:T(8,128)}, u32[]{:S(2)}) copy-start(f32[32,112,256]{2,1,0:T(8,128)} %param.26) | copy-start | bytes 11010052
  147.2 11.9 %copy-start.13 = (f32[112,256]{1,0:T(8,128)S(1)}, f32[112,256]{1,0:T(8,128)}, u32[]{:S(2)}) copy-start(f32[112,256]{1,0:T(8,128)} %param.27) | copy-start | bytes 344068
where the time goes:
time: 166 us; the launch traced here: 163 us
  waiting for transfers between devices  91.5 us (55%)
  matrix products  19.1 us (12%)
  other arithmetic  16.3 us (10%)
  local copies, waits for them, and re-layouts  13.4 us (8%)
  starting transfers between devices  12.5 us (8%)
  blocking collectives  9.35 us (6%)
    ppermute x4, waiting for transfers between devices, passed_along(): return lax.ppermute(array, axis, pairs)  91.5 us
    ppermute x4, starting transfers between devices, passed_along(): return lax.ppermute(array, axis, pairs)  12.5 us
    all_gather x1, blocking collectives, total_of_pieces(): return lax.all_gather(array, axis).sum(0)  9.35 us
    dot_general x2, matrix products, analysis(): jnp.einsum('cxy,vy->cxv', corner_part, matrix_y, precision=lax.Precision....  5.97 us
    unnamed x28, local copies, waits for them, and re-layouts  5.52 us
    dot_general x2, matrix products, analysis(): jnp.einsum('ux,cxv->cuv', matrix_x, corner_part, precision=lax.Precision....  4.6 us
    dot_general x2, matrix products, synthesis(): jnp.einsum('ux,cuv->cxv', matrix_x, corner_part, precision=lax.Precision....  4.51 us
    ppermute x2, local copies, waits for them, and re-layouts, passed_along(): return lax.ppermute(array, axis, pairs)  4.38 us
  transfers between devices with their start and end apart: 4, of which 4 were waited for; matrix products, arithmetic and copies ran while one was open for 1% of the time, Pallas kernels for 0%

commit v1 on v0

v1 whole, which is shorter than its diff:
```python
import functools

import jax
import jax.numpy as jnp
import numpy as np
from jax import lax
from jax.experimental import pallas as pl
from jax.experimental.pallas import tpu as pltpu
from jax.sharding import PartitionSpec as P

LOW_PASS = [
    -0.00011747678400228192,
    0.0006754494059985568,
    -0.0003917403729959771,
    -0.00487035299301066,
    0.008746094047015655,
    0.013981027917015516,
    -0.04408825393106472,
    -0.01736930100202211,
    0.128747426620186,
    0.00047248457399797254,
    -0.2840155429624281,
    -0.015829105256023893,
    0.5853546836548691,
    0.6756307362980128,
    0.3128715909144659,
    0.05441584224308161,
]
TAU_STEP = 0.5
LAMBDA_REG = 1.0
EPSILON = 1e-06
LANES = 128
GROUP = 4
MESH = pl.DeviceIdType.MESH


def level_matrix(length):
    halved = length // 2
    taps_count = len(LOW_PASS)
    matrix = np.zeros((length, length))
    for out_row in range(halved):
        for tap_index in range(taps_count):
            column = (2 * out_row + tap_index) % length
            matrix[out_row, column] += LOW_PASS[tap_index]
            matrix[halved + out_row, column] += (-1) ** tap_index * LOW_PASS[
                taps_count - 1 - tap_index
            ]
    return matrix


def split_np(matrix):
    single = matrix.astype(np.float32)
    high = single.astype(jnp.bfloat16)
    low = (single - high.astype(np.float32)).astype(jnp.bfloat16)
    return np.stack([high, low])


def matrices(ex, ey, border):
    wx, wy = level_matrix(ex), level_matrix(ey)
    hx, hy = ex // 2, ey // 2
    along_y = np.concatenate([level_matrix(hy) @ wy[:hy], wy], axis=0)
    order = np.concatenate([np.arange(border, ey), np.arange(border)])
    along_y = along_y[:, order]
    low_x = np.zeros((2 * ex, ex))
    low_x[:ex, :hx] = (level_matrix(hx) @ wx[:hx]).T
    low_x[ex:, hx:] = wx[hx:].T
    return [
        split_np(low_x),
        split_np(wx.T),
        split_np(along_y),
        split_np(along_y.T),
        split_np(low_x.T),
        split_np(wx),
    ]


def split(value):
    high = value.astype(jnp.bfloat16)
    low = (value - high.astype(jnp.float32)).astype(jnp.bfloat16)
    return high, low


def dot3(a, b):
    dot = functools.partial(jnp.dot, preferred_element_type=jnp.float32)
    return dot(a[0], b[0]) + (dot(a[0], b[1]) + dot(a[1], b[0]))


def kernel(
    sizes,
    img_hbm, grad_hbm, dual_hbm, rw_hbm, lowx_hbm, wxt_hbm, ay_hbm, ayt_hbm, lowxt_hbm, wx_hbm,
    image_next, updated, factor,
    img, grad, dual, rw, lowx, wxt, ay, ayt, lowxt, wx,
    work, fy1_s, fy1_r, fx1_s, fx1_r, fx2_s, fx2_r, fy2_s, fy2_r, total, other,
    dual_sem, img_sem, grad_sem, const_sem,
    fy1_ss, fy1_rs, fx1_ss, fx1_rs, fx2_ss, fx2_rs, fy2_ss, fy2_rs, ch_ss, ch_rs,
):
    n_fx, n_fy, chunks, tx, ty, border = sizes
    ex = tx + border
    tail = ty - LANES
    fx, fy, ch = lax.axis_index("fx"), lax.axis_index("fy"), lax.axis_index("ch")
    has_left, has_right = fx > 0, fx < n_fx - 1
    has_up, has_down = fy > 0, fy < n_fy - 1

    barrier = pltpu.get_barrier_semaphore()

    def greet(condition, where):
        @pl.when(condition)
        def _():
            pl.semaphore_signal(barrier, inc=1, device_id=where, device_id_type=MESH)

    greet(has_left, {"fx": fx - 1})
    greet(has_right, {"fx": fx + 1})
    greet(has_up, {"fy": fy - 1})
    greet(has_down, {"fy": fy + 1})
    pl.semaphore_signal(barrier, inc=1, device_id={"ch": 1 - ch}, device_id_type=MESH)

    def rows_of(k):
        return pl.ds(k * GROUP, GROUP)

    def load(src, dst, sems, k):
        return pltpu.make_async_copy(src.at[rows_of(k)], dst.at[rows_of(k)], sems.at[k])

    constants = [
        (lowx_hbm, lowx), (wxt_hbm, wxt), (ay_hbm, ay), (ayt_hbm, ayt), (lowxt_hbm, lowxt), (wx_hbm, wx), (rw_hbm, rw)
    ]

    def constant(i):
        return pltpu.make_async_copy(constants[i][0], constants[i][1], const_sem.at[i])

    load(dual_hbm, dual, dual_sem, 0).start()
    for i in range(3):
        constant(i).start()
    for k in range(1, chunks):
        load(dual_hbm, dual, dual_sem, k).start()
    for k in range(chunks):
        load(img_hbm, img, img_sem, k).start()
        load(grad_hbm, grad, grad_sem, k).start()
    for i in range(3, len(constants)):
        constant(i).start()

    def clear(condition, ref):
        @pl.when(condition)
        def _():
            ref[...] = jnp.zeros_like(ref)

    clear(fy == n_fy - 1, fy1_r)
    clear(fx == n_fx - 1, fx1_r)
    clear(fx == 0, fx2_r)
    clear(fy == 0, fy2_r)
    total[...] = jnp.zeros_like(total)

    neighbours = (
        has_left.astype(jnp.int32) + has_right.astype(jnp.int32) + has_up.astype(jnp.int32) + has_down.astype(jnp.int32) + 1
    )
    pl.semaphore_wait(barrier, neighbours)

    def remote(src, dst, send, recv, k, where):
        return pltpu.make_async_remote_copy(
            src_ref=src.at[k], dst_ref=dst.at[k], send_sem=send.at[k], recv_sem=recv.at[k],
            device_id=where, device_id_type=MESH,
        )

    def fy1(k):
        return remote(fy1_s, fy1_r, fy1_ss, fy1_rs, k, {"fy": fy - 1})

    def fx1(k):
        return remote(fx1_s, fx1_r, fx1_ss, fx1_rs, k, {"fx": fx - 1})

    def fx2(k):
        return remote(fx2_s, fx2_r, fx2_ss, fx2_rs, k, {"fx": fx + 1})

    def fy2(k):
        return remote(fy2_s, fy2_r, fy2_ss, fy2_rs, k, {"fy": fy + 1})

    lane_e = lax.broadcasted_iota(jnp.int32, (ex, LANES), 1)
    lane_b = lax.broadcasted_iota(jnp.int32, (border, LANES), 1)
    lane_h = lax.broadcasted_iota(jnp.int32, (border // 2, LANES), 1)
    half = border // 2
    low_edge = (lane_e >= tail - border) & (lane_e < tail)

    def pack(strip0, strip1, out, k):
        for c in range(GROUP):
            out[k, c * border : (c + 1) * border, :] = strip0(c)
        tiles = [strip1(c) for c in range(GROUP)]
        for p in range(GROUP // 2):
            at = GROUP * border + p * border
            out[k, at : at + border, :] = jnp.where(lane_b < 64, tiles[2 * p], pltpu.roll(tiles[2 * p + 1], 64, 1))
        rest = jnp.zeros((half, LANES), jnp.float32)
        for c in range(GROUP):
            for part in range(2):
                to = part * 64 + c * 16
                moved = pltpu.roll(tiles[c][part * half : (part + 1) * half], (to - 64) % LANES, 1)
                rest = jnp.where((lane_h >= to) & (lane_h < to + 16), moved, rest)
        at = (GROUP + GROUP // 2) * border
        out[k, at : at + half, :] = rest

    def unpack(ref, k, c):
        first = ref[k, c * border : (c + 1) * border, :]
        at = GROUP * border + (c // 2) * border
        second = ref[k, at : at + border, :]
        if c % 2:
            second = pltpu.roll(second, 64, 1)
        at = (GROUP + GROUP // 2) * border
        rest = ref[k, at : at + half, :]
        parts = []
        for part in range(2):
            shift = (64 - part * 64 - c * 16) % LANES
            parts.append(pltpu.roll(rest, shift, 1) if shift else rest)
        return first, jnp.where(lane_b < 64, second, jnp.concatenate(parts, axis=0))

    def synthesize(k):
        load(dual_hbm, dual, dual_sem, k).wait()
        mat_low, mat_x, mat_y = [(m[0], m[1]) for m in (lowx, wxt, ay)]
        for p in range(GROUP // 2):
            a, b = k * GROUP + 2 * p, k * GROUP + 2 * p + 1
            left = jnp.concatenate([dual[a, :, :LANES], dual[b, :, :LANES]], axis=1)
            right = jnp.concatenate([dual[a, :, LANES:], dual[b, :, LANES:]], axis=1)
            from_left = dot3(mat_low, split(left))
            from_right = dot3(mat_x, split(right))
            tiles = []
            for c, at in ((a, 0), (b, LANES)):
                lanes = slice(at, at + LANES)
                rows = jnp.concatenate([from_left[:ex, lanes], from_left[ex:, lanes], from_right[:, lanes]], axis=1)
                result = dot3(split(rows), mat_y)
                work[c] = result
                tiles.append(result[:, LANES:])
            fy1_s[k, p] = jnp.where(
                low_edge, pltpu.roll(tiles[0], LANES - border, 1), pltpu.roll(tiles[1], 64 - border, 1)
            )
        pl.when(has_up)(lambda: fy1(k).start())

    def send_columns(k):
        pl.when(has_down)(lambda: fy1(k).wait_recv())
        for p in range(GROUP // 2):
            a, b = k * GROUP + 2 * p, k * GROUP + 2 * p + 1
            strip = fy1_r[k, p]
            work[a, :, LANES:] = work[a, :, LANES:] + jnp.where(low_edge, strip, 0.0)
            work[b, :, LANES:] = work[b, :, LANES:] + jnp.where(low_edge, pltpu.roll(strip, 64, 1), 0.0)

        pack(
            lambda c: work[k * GROUP + c, :border, :LANES],
            lambda c: work[k * GROUP + c, :border, LANES:],
            fx1_s, k,
        )
        pl.when(has_left)(lambda: fx1(k).start())

    root = jnp.float32(0.5**0.5)

    def weights(lane_from):
        rows = lax.broadcasted_iota(jnp.int32, (tx, LANES), 0)
        lanes = lax.broadcasted_iota(jnp.int32, (tx, LANES), 1) + lane_from
        by_x = jnp.where((rows >= tx - border) & has_right, root, 1.0)
        by_y = jnp.where((lanes >= ty - border) & has_down, root, 1.0)
        return by_x * by_y

    def update_image(k):
        load(img_hbm, img, img_sem, k).wait()
        load(grad_hbm, grad, grad_sem, k).wait()
        pl.when(has_right)(lambda: fx1(k).wait_recv())
        w0 = weights(0)
        w1 = weights(LANES)[:, :tail]
        for c in range(GROUP):
            i = k * GROUP + c
            add0, add1 = unpack(fx1_r, k, c)
            for own, add, w, lanes in (
                (work[i, border:, :LANES], add0, w0, slice(0, LANES)),
                (work[i, border:, LANES : LANES + tail], add1[:, :tail], w1, slice(LANES, LANES + tail)),
            ):
                keep = tx - border
                summed = jnp.concatenate([own[:keep], own[keep:] + add], axis=0)
                image = img[i, :, lanes]
                step = jnp.maximum(image - TAU_STEP * (grad[i, :, lanes].astype(jnp.float32) + summed * w), 0.0)
                extrap = (2.0 * step - image) * w
                image_next[i, :, lanes] = step
                work[i, border:, lanes] = extrap
        pack(
            lambda c: work[k * GROUP + c, tx:, :LANES],
            lambda c: work[k * GROUP + c, tx:, LANES:],
            fx2_s, k,
        )
        pl.when(has_right)(lambda: fx2(k).start())

    def send_rows(k):
        pl.when(has_left)(lambda: fx2(k).wait_recv())
        for p in range(GROUP // 2):
            tiles = []
            for c in (2 * p, 2 * p + 1):
                i = k * GROUP + c
                add0, add1 = unpack(fx2_r, k, c)
                work[i, :border, :LANES] = add0
                work[i, :border, LANES:] = add1
                tiles.append(jnp.concatenate([add1, work[i, border:, LANES:]], axis=0))
            fy2_s[k, p] = jnp.where(lane_e >= tail, pltpu.roll(tiles[0], border, 1), pltpu.roll(tiles[1], 64 + border, 1))
        pl.when(has_down)(lambda: fy2(k).start())

    def analyse(k):
        pl.when(has_up)(lambda: fy2(k).wait_recv())
        mat_y, mat_low, mat_x = [(m[0], m[1]) for m in (ayt, lowxt, wx)]
        for p in range(GROUP // 2):
            a, b = k * GROUP + 2 * p, k * GROUP + 2 * p + 1
            strip = fy2_r[k, p]
            results = []
            for i, moved in ((a, strip), (b, pltpu.roll(strip, 64, 1))):
                second = jnp.where(lane_e < tail, work[i, :, LANES:], moved)
                window = jnp.concatenate([work[i, :, :LANES], second], axis=1)
                results.append(dot3(split(window), mat_y))
            va, vb = results
            left = jnp.concatenate(
                [
                    jnp.concatenate([va[:, :LANES], vb[:, :LANES]], axis=1),
                    jnp.concatenate([va[:, LANES : 2 * LANES], vb[:, LANES : 2 * LANES]], axis=1),
                ],
                axis=0,
            )
            right = jnp.concatenate([va[:, 2 * LANES :], vb[:, 2 * LANES :]], axis=1)
            low = dot3(mat_low, split(left))
            high = dot3(mat_x, split(right))
            for lanes, part in ((slice(0, LANES), low), (slice(LANES, 2 * LANES), high)):
                first = dual[a, :, lanes] + part[:, :LANES]
                second = dual[b, :, lanes] + part[:, LANES:]
                updated[a, :, lanes] = first
                updated[b, :, lanes] = second
                total[:, lanes] = total[:, lanes] + (first * first + second * second)

    for i in range(len(constants)):
        constant(i).wait()

    phases = ((synthesize, 0), (send_columns, 1), (update_image, 3), (send_rows, 5), (analyse, 6))

    def step(s, carry):
        for phase, lag in phases:

            @pl.when((s >= lag) & (s < chunks + lag))
            def _(phase=phase, lag=lag):
                phase(s - lag)

        return carry

    lax.fori_loop(0, chunks + phases[-1][1], step, 0)

    swap = pltpu.make_async_remote_copy(
        src_ref=total, dst_ref=other, send_sem=ch_ss, recv_sem=ch_rs, device_id={"ch": 1 - ch}, device_id_type=MESH
    )
    swap.start()

    def drain(k, carry):
        pl.when(has_up)(lambda: fy1(k).wait_send())
        pl.when(has_left)(lambda: fx1(k).wait_send())
        pl.when(has_right)(lambda: fx2(k).wait_send())
        pl.when(has_down)(lambda: fy2(k).wait_send())
        return carry

    lax.fori_loop(0, chunks, drain, 0)
    swap.wait()
    factor[...] = jnp.minimum(1.0, LAMBDA_REG * rw[...] / jnp.sqrt(total[...] + other[...] + EPSILON))


def shards(mesh_shape, image_cube, data_grad, dual_coeffs, reweights):
    channels, tx, ty = image_cube.shape
    _, ex, ey = dual_coeffs.shape
    border = ex - tx
    chunks = channels // GROUP
    constants = [jnp.asarray(m) for m in matrices(ex, ey, border)]
    sizes = (mesh_shape["fx"], mesh_shape["fy"], chunks, tx, ty, border)
    f32 = jnp.float32
    strip_y = (chunks, GROUP // 2, ex, LANES)
    strip_x = (chunks, GROUP * border * ty // LANES, LANES)
    dma = pltpu.SemaphoreType.DMA
    in_hbm = pl.BlockSpec(memory_space=pltpu.HBM)
    in_vmem = pl.BlockSpec(memory_space=pltpu.VMEM)
    image_next, updated, factor = pl.pallas_call(
        functools.partial(kernel, sizes),
        out_shape=(
            jax.ShapeDtypeStruct(image_cube.shape, f32),
            jax.ShapeDtypeStruct(dual_coeffs.shape, f32),
            jax.ShapeDtypeStruct(reweights.shape, f32),
        ),
        in_specs=[in_hbm] * (4 + len(constants)),
        out_specs=(in_vmem,) * 3,
        scratch_shapes=[
            pltpu.VMEM(image_cube.shape, f32),
            pltpu.VMEM(data_grad.shape, data_grad.dtype),
            pltpu.VMEM(dual_coeffs.shape, f32),
            pltpu.VMEM(reweights.shape, f32),
            *[pltpu.VMEM(m.shape, m.dtype) for m in constants],
            pltpu.VMEM(dual_coeffs.shape, f32),
            pltpu.VMEM(strip_y, f32), pltpu.VMEM(strip_y, f32),
            pltpu.VMEM(strip_x, f32), pltpu.VMEM(strip_x, f32),
            pltpu.VMEM(strip_x, f32), pltpu.VMEM(strip_x, f32),
            pltpu.VMEM(strip_y, f32), pltpu.VMEM(strip_y, f32),
            pltpu.VMEM((ex, ey), f32), pltpu.VMEM((ex, ey), f32),
            dma((chunks,)), dma((chunks,)), dma((chunks,)), dma((7,)),
            *[dma((chunks,)) for _ in range(8)],
            dma, dma,
        ],
        compiler_params=pltpu.CompilerParams(
            collective_id=0, has_side_effects=True, vmem_limit_bytes=40 * 2**20
        ),
        name="primal_dual",
    )(*[pltpu.with_memory_space_constraint(x, pltpu.HBM) for x in (image_cube, data_grad, dual_coeffs, reweights, *constants)])
    return image_next, updated * factor[None]


def solution(mesh):
    return jax.shard_map(
        functools.partial(shards, dict(mesh.shape)),
        mesh=mesh,
        in_specs=(P("ch", "fx", "fy"), P("ch", "fx", "fy"), P("ch", "fx", "fy"), P("fx", "fy")),
        out_specs=(P("ch", "fx", "fy"), P("ch", "fx", "fy")),
        check_vma=False,
    )
```

time: 166 us -> 85.5 us (0.52)
  waiting for transfers between devices: 91.5 us -> 0 us
  Pallas kernels: 0 us -> 80.1 us
  matrix products: 19.1 us -> 0 us
  other arithmetic: 16.3 us -> 2.11 us
  starting transfers between devices: 12.5 us -> 0 us
  local copies, waits for them, and re-layouts: 13.4 us -> 1.32 us
  blocking collectives: 9.35 us -> 0 us
    ppermute x4 -> x0, waiting for transfers between devices: 91.5 us -> none  [passed_along(): return lax.ppermute(array, axis, pairs)]
    pallas_call x0 -> x1, Pallas kernels: none -> 80.1 us  [shards(): pl.pallas_call(functools.partial(kernel, sizes), out_shape=(jax.ShapeDtyp...]
    dot_general x8 -> x0, matrix products: 19.1 us -> none  [the longest x2 5.97 us: analysis(): jnp.einsum('cxy,vy->cxv', corner_part, matrix_y, precision=lax.Precision....]
    ppermute x4 -> x0, starting transfers between devices: 12.5 us -> none  [passed_along(): return lax.ppermute(array, axis, pairs)]
    all_gather x1 -> x0, blocking collectives: 9.35 us -> none  [total_of_pieces(): return lax.all_gather(array, axis).sum(0)]
    mul x3 -> x1, other arithmetic: 7.59 us -> 2.11 us  [shards(): return (image_next, updated * factor[None])]
    ppermute x2 -> x0, local copies, waits for them, and re-layouts: 4.38 us -> none  [passed_along(): return lax.ppermute(array, axis, pairs)]
    unnamed x28 -> x1, local copies, waits for them, and re-layouts: 5.52 us -> 1.32 us
  transfers between devices with their start and end apart: 4 -> 0, of which waited for: 4 -> 0; matrix products, arithmetic and copies ran while one was open for 1% -> 0% of each run, Pallas kernels for 0% -> 0%
where the time goes in v1:
time: 85.5 us; the launch traced here: 84.2 us
  Pallas kernels  80.1 us (94%)
  other arithmetic  2.11 us (2%)
  local copies, waits for them, and re-layouts  1.32 us (2%)
    pallas_call x1, Pallas kernels, shards(): pl.pallas_call(functools.partial(kernel, sizes), out_shape=(jax.ShapeDtyp...  80.1 us
    mul x1, other arithmetic, shards(): return (image_next, updated * factor[None])  2.11 us

profile of v1, /device:TPU:22, one launch (start us, length us, event | category | flops | bytes accessed | tf_op | source)
XLA Modules:
  0.0 84.2 jit_solution(17826740184400326587)
XLA Ops:
  0.6 80.1 %primal_dual.1 = (f32[32,64,208]{2,1,0:T(8,128)S(1)}, f32[32,112,256]{2,1,0:T(8,128)S(1)}, f32[112,256]{1,0:T(8,128)S(1)}) custom-call(f32[32,64,208]{2,1,0:T(8,128)} %img_hbm.1, bf16[32,64,208]{2,1,0:T(8,128)(2,1)} %grad_hbm.1, f32[32,112,256]{2,1,0:T(8,128)} %dual_hbm.1, f32[112,256]{1,0:T(8,128)} %rw_hbm.1, bf16[2,224,112]{2,1,0:T(8,128)(2,1)} %constant.12.clone.lowx_hbm, ...), custom_call_target="tpu_custom_call" | custom-call | tf_op jit(solution)/shard_map/primal_dual/pallas_call | solution.py:371
  80.8 2.1 %broadcast_multiply_fusion = f32[32,112,256]{2,1,0:T(8,128)} fusion(f32[32,112,256]{2,1,0:T(8,128)S(1)} %get-tuple-element.6, f32[112,256]{1,0:T(8,128)S(1)} %get-tuple-element.7), kind=kLoop, calls=%fused_computation | loop fusion | flops 917504 | bytes 7454720 | tf_op jit(solution)/shard_map/mul | solution.py:401
  82.9 1.3 %copy.13 = f32[32,64,208]{2,1,0:T(8,128)} copy(f32[32,64,208]{2,1,0:T(8,128)S(1)} %get-tuple-element.10) | data formatting | bytes 3407872

commit v2 on v1

v2 whole, which is shorter than its diff:
```python
import functools

import jax
import jax.numpy as jnp
import numpy as np
from jax import lax
from jax.experimental import pallas as pl
from jax.experimental.pallas import tpu as pltpu
from jax.sharding import PartitionSpec as P

LOW_PASS = [
    -0.00011747678400228192,
    0.0006754494059985568,
    -0.0003917403729959771,
    -0.00487035299301066,
    0.008746094047015655,
    0.013981027917015516,
    -0.04408825393106472,
    -0.01736930100202211,
    0.128747426620186,
    0.00047248457399797254,
    -0.2840155429624281,
    -0.015829105256023893,
    0.5853546836548691,
    0.6756307362980128,
    0.3128715909144659,
    0.05441584224308161,
]
TAU_STEP = 0.5
LAMBDA_REG = 1.0
EPSILON = 1e-06
LANES = 128
GROUP = 4
MESH = pl.DeviceIdType.MESH


def level_matrix(length):
    halved = length // 2
    taps_count = len(LOW_PASS)
    matrix = np.zeros((length, length))
    for out_row in range(halved):
        for tap_index in range(taps_count):
            column = (2 * out_row + tap_index) % length
            matrix[out_row, column] += LOW_PASS[tap_index]
            matrix[halved + out_row, column] += (-1) ** tap_index * LOW_PASS[
                taps_count - 1 - tap_index
            ]
    return matrix


def split_np(matrix):
    single = matrix.astype(np.float32)
    high = single.astype(jnp.bfloat16)
    low = (single - high.astype(np.float32)).astype(jnp.bfloat16)
    return np.stack([high, low])


def matrices(ex, ey, border):
    wx, wy = level_matrix(ex), level_matrix(ey)
    hx, hy = ex // 2, ey // 2
    along_y = np.concatenate([level_matrix(hy) @ wy[:hy], wy], axis=0)
    order = np.concatenate([np.arange(border, ey), np.arange(border)])
    along_y = along_y[:, order]
    low_x = np.zeros((2 * ex, ex))
    low_x[:ex, :hx] = (level_matrix(hx) @ wx[:hx]).T
    low_x[ex:, hx:] = wx[hx:].T
    return [
        split_np(low_x),
        split_np(wx.T),
        split_np(along_y),
        split_np(along_y.T),
        split_np(low_x.T),
        split_np(wx),
    ]


def split(value):
    high = value.astype(jnp.bfloat16)
    low = (value - high.astype(jnp.float32)).astype(jnp.bfloat16)
    return high, low


def dot3(a, b):
    dot = functools.partial(jnp.dot, preferred_element_type=jnp.float32)
    return dot(a[0], b[0]) + (dot(a[0], b[1]) + dot(a[1], b[0]))


def kernel(
    sizes,
    img_hbm, grad_hbm, dual_hbm, rw_hbm, lowx_hbm, wxt_hbm, ay_hbm, ayt_hbm, lowxt_hbm, wx_hbm,
    image_next, updated, factor,
    img, grad, dual, rw, lowx, wxt, ay, ayt, lowxt, wx,
    work, rows_hi, rows_lo, mixed,
    fy1_s, fy1_r, bulk1_s, bulk1_r, corner1_s, corner1_r,
    bulk2_s, bulk2_r, corner2_s, corner2_r, fy2_s, fy2_r, total, other,
    dual_sem, img_sem, grad_sem, const_sem,
    fy1_ss, fy1_rs, bulk1_ss, bulk1_rs, corner1_ss, corner1_rs,
    bulk2_ss, bulk2_rs, corner2_ss, corner2_rs, fy2_ss, fy2_rs, ch_ss, ch_rs,
):
    n_fx, n_fy, chunks, tx, ty, border = sizes
    ex = tx + border
    ey = ty + border
    tail = ty - LANES
    half = border // 2
    fx, fy, ch = lax.axis_index("fx"), lax.axis_index("fy"), lax.axis_index("ch")
    has_left, has_right = fx > 0, fx < n_fx - 1
    has_up, has_down = fy > 0, fy < n_fy - 1

    barrier = pltpu.get_barrier_semaphore()

    def greet(condition, where):
        @pl.when(condition)
        def _():
            pl.semaphore_signal(barrier, inc=1, device_id=where, device_id_type=MESH)

    greet(has_left, {"fx": fx - 1})
    greet(has_right, {"fx": fx + 1})
    greet(has_up, {"fy": fy - 1})
    greet(has_down, {"fy": fy + 1})
    pl.semaphore_signal(barrier, inc=1, device_id={"ch": 1 - ch}, device_id_type=MESH)
    neighbours = 1 + sum(c.astype(jnp.int32) for c in (has_left, has_right, has_up, has_down))

    def load(src, dst, sems, k):
        rows = pl.ds(k * GROUP, GROUP)
        return pltpu.make_async_copy(src.at[rows], dst.at[rows], sems.at[k])

    constants = [
        (lowx_hbm, lowx), (wxt_hbm, wxt), (ay_hbm, ay), (ayt_hbm, ayt), (lowxt_hbm, lowxt), (wx_hbm, wx), (rw_hbm, rw)
    ]

    def constant(i):
        return pltpu.make_async_copy(constants[i][0], constants[i][1], const_sem.at[i])

    load(dual_hbm, dual, dual_sem, 0).start()
    for i in range(3):
        constant(i).start()
    for k in range(1, chunks):
        load(dual_hbm, dual, dual_sem, k).start()
    for k in range(chunks):
        load(img_hbm, img, img_sem, k).start()
        load(grad_hbm, grad, grad_sem, k).start()
    for i in range(3, len(constants)):
        constant(i).start()

    def clear(condition, *refs):
        @pl.when(condition)
        def _():
            for ref in refs:
                ref[...] = jnp.zeros_like(ref)

    clear(fy == n_fy - 1, fy1_r)
    clear(fx == n_fx - 1, bulk1_r, corner1_r)
    clear(fx == 0, bulk2_r, corner2_r)
    clear(fy == 0, fy2_r)
    total[...] = jnp.zeros_like(total)

    def remote(src, dst, send, recv, k, where):
        return pltpu.make_async_remote_copy(
            src_ref=src.at[k], dst_ref=dst.at[k], send_sem=send.at[k], recv_sem=recv.at[k],
            device_id=where, device_id_type=MESH,
        )

    def fy1(k):
        return remote(fy1_s, fy1_r, fy1_ss, fy1_rs, k, {"fy": fy - 1})

    def bulk1(k):
        return remote(bulk1_s, bulk1_r, bulk1_ss, bulk1_rs, k, {"fx": fx - 1})

    def corner1(k):
        return remote(corner1_s, corner1_r, corner1_ss, corner1_rs, k, {"fx": fx - 1})

    def bulk2(k):
        return remote(bulk2_s, bulk2_r, bulk2_ss, bulk2_rs, k, {"fx": fx + 1})

    def corner2(k):
        return remote(corner2_s, corner2_r, corner2_ss, corner2_rs, k, {"fx": fx + 1})

    def fy2(k):
        return remote(fy2_s, fy2_r, fy2_ss, fy2_rs, k, {"fy": fy + 1})

    lane_e = lax.broadcasted_iota(jnp.int32, (ex, LANES), 1)
    lane_b = lax.broadcasted_iota(jnp.int32, (border, LANES), 1)
    lane_h = lax.broadcasted_iota(jnp.int32, (half, LANES), 1)
    low_edge = (lane_e >= tail - border) & (lane_e < tail)

    def roll(value, shift):
        shift = shift % LANES
        return pltpu.roll(value, shift, 1) if shift else value

    def pack_bulk(tile0, tile1, out, k):
        joined = jnp.zeros((border, LANES), jnp.float32)
        for c in range(GROUP):
            out[k, c * border : (c + 1) * border, :] = tile0(c)
            moved = roll(tile1(c), 32 * c)
            joined = jnp.where((lane_b >= 32 * c) & (lane_b < 32 * c + 32), moved, joined)
        out[k, GROUP * border : (GROUP + 1) * border, :] = joined

    def pack_corner(tile1, out, k):
        joined = jnp.zeros((border, LANES), jnp.float32)
        rest = jnp.zeros((half, LANES), jnp.float32)
        for c in range(GROUP):
            value = tile1(c)
            moved = roll(value, 32 * c - 32)
            joined = jnp.where((lane_b >= 32 * c) & (lane_b < 32 * c + 32), moved, joined)
            for part in range(2):
                to = part * 64 + c * 16
                moved = roll(value[part * half : (part + 1) * half], to - 64)
                rest = jnp.where((lane_h >= to) & (lane_h < to + 16), moved, rest)
        out[k, :border, :] = joined
        out[k, border:, :] = rest

    def unpack_corner(ref, k, c):
        middle = roll(ref[k, :border, :], 32 - 32 * c)
        parts = [roll(ref[k, border:, :], 64 - part * 64 - c * 16) for part in range(2)]
        return jnp.where(lane_b < 64, middle, jnp.concatenate(parts, axis=0))

    def unpack(bulk, corner, k, c):
        first = bulk[k, c * border : (c + 1) * border, :]
        start = roll(bulk[k, GROUP * border : (GROUP + 1) * border, :], -32 * c)
        return first, jnp.where(lane_b < 32, start, unpack_corner(corner, k, c))

    def put_rows(at, lanes, value):
        high = value.astype(jnp.bfloat16)
        rows_hi[at : at + ex, lanes] = high
        rows_lo[at : at + ex, lanes] = (value - high.astype(jnp.float32)).astype(jnp.bfloat16)

    def synthesize(k):
        load(dual_hbm, dual, dual_sem, k).wait()
        first = k * GROUP
        left = jnp.concatenate([dual[first + c, :, :LANES] for c in range(GROUP)], axis=1)
        from_left = dot3((lowx[0], lowx[1]), split(left))
        for c in range(GROUP):
            lanes = slice(c * LANES, (c + 1) * LANES)
            put_rows(c * ex, slice(0, LANES), from_left[:ex, lanes])
            put_rows(c * ex, slice(LANES, 2 * LANES), from_left[ex:, lanes])
        right = jnp.concatenate([dual[first + c, :, LANES:] for c in range(GROUP)], axis=1)
        from_right = dot3((wxt[0], wxt[1]), split(right))
        for c in range(GROUP):
            put_rows(c * ex, slice(2 * LANES, 3 * LANES), from_right[:, c * LANES : (c + 1) * LANES])
        result = dot3((rows_hi[...], rows_lo[...]), (ay[0], ay[1]))
        for c in range(GROUP):
            work[first + c] = result[c * ex : (c + 1) * ex]

        @pl.when(k == 0)
        def _():
            pl.semaphore_wait(barrier, neighbours)

        for p in range(GROUP // 2):
            a, b = work[first + 2 * p, :, LANES:], work[first + 2 * p + 1, :, LANES:]
            fy1_s[k, p] = jnp.where(low_edge, roll(a, -border), roll(b, 64 - border))
        pl.when(has_up)(lambda: fy1(k).start())
        pack_bulk(
            lambda c: work[first + c, :border, :LANES], lambda c: work[first + c, :border, LANES:], bulk1_s, k
        )
        pl.when(has_left)(lambda: bulk1(k).start())

    def send_columns(k):
        pl.when(has_down)(lambda: fy1(k).wait_recv())
        for p in range(GROUP // 2):
            a = k * GROUP + 2 * p
            strip = fy1_r[k, p]
            work[a, :, LANES:] = work[a, :, LANES:] + jnp.where(low_edge, strip, 0.0)
            work[a + 1, :, LANES:] = work[a + 1, :, LANES:] + jnp.where(low_edge, roll(strip, 64), 0.0)
        pack_corner(lambda c: work[k * GROUP + c, :border, LANES:], corner1_s, k)
        pl.when(has_left)(lambda: corner1(k).start())

    root = jnp.float32(0.5**0.5)

    def weights(lane_from):
        rows = lax.broadcasted_iota(jnp.int32, (tx, LANES), 0)
        lanes = lax.broadcasted_iota(jnp.int32, (tx, LANES), 1) + lane_from
        by_x = jnp.where((rows >= tx - border) & has_right, root, 1.0)
        by_y = jnp.where((lanes >= ty - border) & has_down, root, 1.0)
        return by_x * by_y

    def update_image(k):
        load(img_hbm, img, img_sem, k).wait()
        load(grad_hbm, grad, grad_sem, k).wait()

        @pl.when(has_right)
        def _():
            bulk1(k).wait_recv()
            corner1(k).wait_recv()

        keep = tx - border
        w0 = weights(0)
        w1 = weights(LANES)[:, :tail]
        for c in range(GROUP):
            i = k * GROUP + c
            add0, add1 = unpack(bulk1_r, corner1_r, k, c)
            for own, add, w, lanes in (
                (work[i, border:, :LANES], add0, w0, slice(0, LANES)),
                (work[i, border:, LANES:ty], add1[:, :tail], w1, slice(LANES, ty)),
            ):
                summed = jnp.concatenate([own[:keep], own[keep:] + add], axis=0)
                image = img[i, :, lanes]
                step = jnp.maximum(image - TAU_STEP * (grad[i, :, lanes].astype(jnp.float32) + summed * w), 0.0)
                image_next[i, :, lanes] = step
                work[i, border:, lanes] = (2.0 * step - image) * w
        pack_corner(lambda c: work[k * GROUP + c, tx:, LANES:], corner2_s, k)
        pl.when(has_right)(lambda: corner2(k).start())
        pack_bulk(
            lambda c: work[k * GROUP + c, tx:, :LANES], lambda c: work[k * GROUP + c, tx:, LANES:], bulk2_s, k
        )
        pl.when(has_right)(lambda: bulk2(k).start())

    def send_rows(k):
        pl.when(has_left)(lambda: corner2(k).wait_recv())
        for p in range(GROUP // 2):
            a, b = [
                jnp.concatenate([unpack_corner(corner2_r, k, c), work[k * GROUP + c, border:, LANES:]], axis=0)
                for c in (2 * p, 2 * p + 1)
            ]
            fy2_s[k, p] = jnp.where(lane_e >= tail, roll(a, border), roll(b, 64 + border))
        pl.when(has_down)(lambda: fy2(k).start())

    def analyse(k):
        @pl.when(k == 0)
        def _():
            for i in range(3, len(constants)):
                constant(i).wait()

        pl.when(has_left)(lambda: bulk2(k).wait_recv())
        pl.when(has_up)(lambda: fy2(k).wait_recv())
        first = k * GROUP
        for c in range(GROUP):
            i = first + c
            strip = roll(fy2_r[k, c // 2], 64 * (c % 2))
            edge0, edge1 = unpack(bulk2_r, corner2_r, k, c)
            put_rows(c * ex, slice(0, LANES), jnp.concatenate([edge0, work[i, border:, :LANES]], axis=0))
            second = jnp.concatenate([edge1, work[i, border:, LANES:]], axis=0)
            put_rows(c * ex, slice(LANES, 2 * LANES), jnp.where(lane_e < tail, second, strip))
        mixed[...] = dot3((rows_hi[:, :ey], rows_lo[:, :ey]), (ayt[0], ayt[1]))

        def beside(tile):
            lanes = slice(tile * LANES, (tile + 1) * LANES)
            return jnp.concatenate([mixed[c * ex : (c + 1) * ex, lanes] for c in range(GROUP)], axis=1)

        low = dot3((lowxt[0], lowxt[1]), split(jnp.concatenate([beside(0), beside(1)], axis=0)))
        high = dot3((wx[0], wx[1]), split(beside(2)))
        for lanes, part in ((slice(0, LANES), low), (slice(LANES, 2 * LANES), high)):
            squares = total[:, lanes]
            for c in range(GROUP):
                value = dual[first + c, :, lanes] + part[:, c * LANES : (c + 1) * LANES]
                updated[first + c, :, lanes] = value
                squares = squares + value * value
            total[:, lanes] = squares

    for i in range(3):
        constant(i).wait()

    phases = ((synthesize, 0), (send_columns, 1), (update_image, 3), (send_rows, 5), (analyse, 6))

    def step(s, carry):
        for phase, lag in phases:

            @pl.when((s >= lag) & (s < chunks + lag))
            def _(phase=phase, lag=lag):
                phase(s - lag)

        return carry

    lax.fori_loop(0, chunks + phases[-1][1], step, 0)

    swap = pltpu.make_async_remote_copy(
        src_ref=total, dst_ref=other, send_sem=ch_ss, recv_sem=ch_rs, device_id={"ch": 1 - ch}, device_id_type=MESH
    )
    swap.start()

    def drain(k, carry):
        pl.when(has_up)(lambda: fy1(k).wait_send())

        @pl.when(has_left)
        def _():
            bulk1(k).wait_send()
            corner1(k).wait_send()

        @pl.when(has_right)
        def _():
            bulk2(k).wait_send()
            corner2(k).wait_send()

        pl.when(has_down)(lambda: fy2(k).wait_send())
        return carry

    lax.fori_loop(0, chunks, drain, 0)
    swap.wait()
    factor[...] = jnp.minimum(1.0, LAMBDA_REG * rw[...] / jnp.sqrt(total[...] + other[...] + EPSILON))


def finish(chunks, image, updated, factor, image_out, dual_out, scaled, image_sem, sems):
    pltpu.make_async_copy(image, image_out, image_sem).start()

    def copy(k):
        rows = pl.ds(k * GROUP, GROUP)
        return pltpu.make_async_copy(scaled.at[rows], dual_out.at[rows], sems.at[k])

    def step(k, carry):
        for c in range(GROUP):
            scaled[k * GROUP + c] = updated[k * GROUP + c] * factor[...]
        copy(k).start()
        return carry

    lax.fori_loop(0, chunks, step, 0)
    pltpu.make_async_copy(image, image_out, image_sem).wait()

    def drain(k, carry):
        copy(k).wait()
        return carry

    lax.fori_loop(0, chunks, drain, 0)


def shards(mesh_shape, image_cube, data_grad, dual_coeffs, reweights):
    channels, tx, ty = image_cube.shape
    _, ex, ey = dual_coeffs.shape
    border = ex - tx
    chunks = channels // GROUP
    constants = [jnp.asarray(m) for m in matrices(ex, ey, border)]
    sizes = (mesh_shape["fx"], mesh_shape["fy"], chunks, tx, ty, border)
    f32, bf16 = jnp.float32, jnp.bfloat16
    strip_y = pltpu.VMEM((chunks, GROUP // 2, ex, LANES), f32)
    bulk = pltpu.VMEM((chunks, (GROUP + 1) * border, LANES), f32)
    corner = pltpu.VMEM((chunks, border + border // 2, LANES), f32)
    dma = pltpu.SemaphoreType.DMA
    in_hbm = pl.BlockSpec(memory_space=pltpu.HBM)
    in_vmem = pl.BlockSpec(memory_space=pltpu.VMEM)
    operands = [
        pltpu.with_memory_space_constraint(x, pltpu.HBM)
        for x in (image_cube, data_grad, dual_coeffs, reweights, *constants)
    ]
    image_next, updated, factor = pl.pallas_call(
        functools.partial(kernel, sizes),
        out_shape=(
            jax.ShapeDtypeStruct(image_cube.shape, f32),
            jax.ShapeDtypeStruct(dual_coeffs.shape, f32),
            jax.ShapeDtypeStruct(reweights.shape, f32),
        ),
        in_specs=[in_hbm] * len(operands),
        out_specs=(in_vmem,) * 3,
        scratch_shapes=[
            pltpu.VMEM(image_cube.shape, f32),
            pltpu.VMEM(data_grad.shape, data_grad.dtype),
            pltpu.VMEM(dual_coeffs.shape, f32),
            pltpu.VMEM(reweights.shape, f32),
            *[pltpu.VMEM(m.shape, m.dtype) for m in constants],
            pltpu.VMEM(dual_coeffs.shape, f32),
            pltpu.VMEM((GROUP * ex, ey + LANES), bf16),
            pltpu.VMEM((GROUP * ex, ey + LANES), bf16),
            pltpu.VMEM((GROUP * ex, ey + LANES), f32),
            strip_y, strip_y, bulk, bulk, corner, corner, bulk, bulk, corner, corner, strip_y, strip_y,
            pltpu.VMEM((ex, ey), f32), pltpu.VMEM((ex, ey), f32),
            dma((chunks,)), dma((chunks,)), dma((chunks,)), dma((7,)),
            *[dma((chunks,)) for _ in range(12)],
            dma, dma,
        ],
        compiler_params=pltpu.CompilerParams(
            collective_id=0, has_side_effects=True, vmem_limit_bytes=40 * 2**20
        ),
        name="primal_dual",
    )(*operands)
    return pl.pallas_call(
        functools.partial(finish, chunks),
        out_shape=(
            jax.ShapeDtypeStruct(image_cube.shape, f32),
            jax.ShapeDtypeStruct(dual_coeffs.shape, f32),
        ),
        in_specs=[in_vmem] * 3,
        out_specs=(in_hbm,) * 2,
        scratch_shapes=[pltpu.VMEM(dual_coeffs.shape, f32), dma, dma((chunks,))],
        compiler_params=pltpu.CompilerParams(vmem_limit_bytes=16 * 2**20),
        name="scaled_results",
    )(image_next, updated, factor)


def solution(mesh):
    return jax.shard_map(
        functools.partial(shards, dict(mesh.shape)),
        mesh=mesh,
        in_specs=(P("ch", "fx", "fy"), P("ch", "fx", "fy"), P("ch", "fx", "fy"), P("fx", "fy")),
        out_specs=(P("ch", "fx", "fy"), P("ch", "fx", "fy")),
        check_vma=False,
    )
```

time: 85.5 us -> 79.1 us (0.925); the launches traced: 84.2 us -> 78.8 us
  other arithmetic: 2.11 us -> 0 us
  Pallas kernels: 80.1 us -> 78.2 us
  local copies, waits for them, and re-layouts: 1.32 us -> 0 us
    pallas_call x1, Pallas kernels: 80.1 us -> 75.6 us  [shards(): pl.pallas_call(functools.partial(kernel, sizes), out_shape=(jax.ShapeDtyp...]
    pallas_call x0 -> x1, Pallas kernels: none -> 2.57 us  [shards(): pl.pallas_call(functools.partial(finish, chunks), out_shape=(jax.ShapeDty...]
    mul x1 -> x0, other arithmetic: 2.11 us -> none  [shards(): return (image_next, updated * factor[None])]
    unnamed x1 -> x0, local copies, waits for them, and re-layouts: 1.32 us -> none
where the time goes in v2:
time: 79.1 us; the launch traced here: 78.8 us
  Pallas kernels  78.2 us (99%)
    pallas_call x1, Pallas kernels, shards(): pl.pallas_call(functools.partial(kernel, sizes), out_shape=(jax.ShapeDtyp...  75.6 us
    pallas_call x1, Pallas kernels, shards(): pl.pallas_call(functools.partial(finish, chunks), out_shape=(jax.ShapeDty...  2.57 us

profile of v2, /device:TPU:22, one launch (start us, length us, event | category | flops | bytes accessed | tf_op | source)
XLA Modules:
  0.0 78.8 jit_solution(4721731604943400511)
XLA Ops:
  0.6 75.6 %primal_dual.1 = (f32[32,64,208]{2,1,0:T(8,128)S(1)}, f32[32,112,256]{2,1,0:T(8,128)S(1)}, f32[112,256]{1,0:T(8,128)S(1)}) custom-call(f32[32,64,208]{2,1,0:T(8,128)} %img_hbm.1, bf16[32,64,208]{2,1,0:T(8,128)(2,1)} %grad_hbm.1, f32[32,112,256]{2,1,0:T(8,128)} %dual_hbm.1, f32[112,256]{1,0:T(8,128)} %rw_hbm.1, bf16[2,224,112]{2,1,0:T(8,128)(2,1)} %constant.12.clone.lowx_hbm, ...), custom_call_target="tpu_custom_call" | custom-call | tf_op jit(solution)/shard_map/primal_dual/pallas_call | solution.py:432
  76.3 2.6 %scaled_results.1 = (f32[32,64,208]{2,1,0:T(8,128)}, f32[32,112,256]{2,1,0:T(8,128)}) custom-call(f32[32,64,208]{2,1,0:T(8,128)S(1)} %get-tuple-element.5.image, f32[32,112,256]{2,1,0:T(8,128)S(1)} %get-tuple-element.6.updated, f32[112,256]{1,0:T(8,128)S(1)} %get-tuple-element.7.factor), custom_call_target="tpu_custom_call" | custom-call | tf_op jit(solution)/shard_map/scaled_results/pallas_call | solution.py:462

commit v3 on v2

--- a/solution.py
+++ b/solution.py
@@ -31,6 +31,12 @@
 EPSILON = 1e-06
 LANES = 128
 GROUP = 4
+RUN = 4
+RELAYED_LEFT = ((0, 1, 3, 4, 6), (1, 3, 5), (3,))
+RELAYED_RIGHT = ((2, 6), (0, 2, 4, 6), (0, 1, 2, 4, 5, 6))
+IMAGE_LAG = (5, 8)
+ROWS_LAG = (13, 16)
+RELAY_LAG = (3, 7)
 MESH = pl.DeviceIdType.MESH
 
 
@@ -92,10 +98,11 @@
     img, grad, dual, rw, lowx, wxt, ay, ayt, lowxt, wx,
     work, rows_hi, rows_lo, mixed,
     fy1_s, fy1_r, bulk1_s, bulk1_r, corner1_s, corner1_r,
-    bulk2_s, bulk2_r, corner2_s, corner2_r, fy2_s, fy2_r, total, other,
+    bulk2_s, bulk2_r, corner2_s, corner2_r, fy2_s, fy2_r, via_bulk, via_corner, total, other,
     dual_sem, img_sem, grad_sem, const_sem,
     fy1_ss, fy1_rs, bulk1_ss, bulk1_rs, corner1_ss, corner1_rs,
-    bulk2_ss, bulk2_rs, corner2_ss, corner2_rs, fy2_ss, fy2_rs, ch_ss, ch_rs,
+    bulk2_ss, bulk2_rs, corner2_ss, corner2_rs, fy2_ss, fy2_rs,
+    via_bulk_ss, via_bulk_rs, via_corner_ss, via_corner_rs, ch_ss, ch_rs,
 ):
     n_fx, n_fy, chunks, tx, ty, border = sizes
     ex = tx + border
@@ -106,6 +113,34 @@
     has_left, has_right = fx > 0, fx < n_fx - 1
     has_up, has_down = fy > 0, fy < n_fy - 1
 
+    relays = n_fx == RUN * RUN
+    run, place = fx // RUN, fx % RUN
+    at_first, at_last = place == 0, place == RUN - 1
+    if relays:
+        crosses_left, crosses_right = at_first & has_left, at_last & has_right
+        via1_here, via2_here = at_first & (run < RUN - 1), at_last & (run > 0)
+    else:
+        crosses_left = crosses_right = via1_here = via2_here = False
+
+    def among(chosen, pair, k):
+        found = False
+        for index, listed in enumerate(chosen):
+            for member in listed:
+                found = found | ((pair == index) & (k == member))
+        return found
+
+    def by_relay(crosses, relayed, direct, relay, action):
+        if not relays:
+            return action(direct())
+        pl.when(crosses & relayed)(lambda: action(relay()))
+        pl.when(jnp.logical_not(crosses & relayed))(lambda: action(direct()))
+
+    def left_relayed(k):
+        return among(RELAYED_LEFT, run - 1, k)
+
+    def right_relayed(k):
+        return among(RELAYED_RIGHT, run, k)
+
     barrier = pltpu.get_barrier_semaphore()
 
     def greet(condition, where):
@@ -119,6 +154,13 @@
     greet(has_down, {"fy": fy + 1})
     pl.semaphore_signal(barrier, inc=1, device_id={"ch": 1 - ch}, device_id_type=MESH)
     neighbours = 1 + sum(c.astype(jnp.int32) for c in (has_left, has_right, has_up, has_down))
+    if relays:
+        ends = at_first | at_last
+        for condition, offset in (
+            (ends & (run > 0), -RUN), (ends & (run < RUN - 1), RUN), (at_first, RUN - 1), (at_last, 1 - RUN)
+        ):
+            greet(condition, {"fx": fx + offset})
+            neighbours = neighbours + condition.astype(jnp.int32)
 
     def load(src, dst, sems, k):
         rows = pl.ds(k * GROUP, GROUP)
@@ -134,14 +176,6 @@
     load(dual_hbm, dual, dual_sem, 0).start()
     for i in range(3):
         constant(i).start()
-    for k in range(1, chunks):
-        load(dual_hbm, dual, dual_sem, k).start()
-    for k in range(chunks):
-        load(img_hbm, img, img_sem, k).start()
-        load(grad_hbm, grad, grad_sem, k).start()
-    for i in range(3, len(constants)):
-        constant(i).start()
-
     def clear(condition, *refs):
         @pl.when(condition)
         def _():
@@ -174,6 +208,67 @@
 
     def corner2(k):
         return remote(corner2_s, corner2_r, corner2_ss, corner2_rs, k, {"fx": fx + 1})
+
+    def to_relay(src, via, send, recv, k, offset):
+        return remote(src, via, send, recv, k, {"fx": fx + offset})
+
+    def via_bulk1(k):
+        return to_relay(bulk1_s, via_bulk, bulk1_ss, via_bulk_rs, k, -RUN)
+
+    def via_corner1(k):
+        return to_relay(corner1_s, via_corner, corner1_ss, via_corner_rs, k, -RUN)
+
+    def via_bulk2(k):
+        return to_relay(bulk2_s, via_bulk, bulk2_ss, via_bulk_rs, k, RUN)
+
+    def via_corner2(k):
+        return to_relay(corner2_s, via_corner, corner2_ss, via_corner_rs, k, RUN)
+
+    def on_bulk1(k):
+        return to_relay(via_bulk, bulk1_r, via_bulk_ss, bulk1_rs, k, RUN - 1)
+
+    def on_corner1(k):
+        return to_relay(via_corner, corner1_r, via_corner_ss, corner1_rs, k, RUN - 1)
+
+    def on_bulk2(k):
+        return to_relay(via_bulk, bulk2_r, via_bulk_ss, bulk2_rs, k, 1 - RUN)
+
+    def on_corner2(k):
+        return to_relay(via_corner, corner2_r, via_corner_ss, corner2_rs, k, 1 - RUN)
+
+    def leftward(direct, relay, k, action):
+        pl.when(has_left)(lambda: by_relay(crosses_left, left_relayed(k), lambda: direct(k), lambda: relay(k), action))
+
+    def rightward(direct, relay, k, action):
+        pl.when(has_right)(lambda: by_relay(crosses_right, right_relayed(k), lambda: direct(k), lambda: relay(k), action))
+
+    def start(copy):
+        copy.start()
+
+    def wait_send(copy):
+        copy.wait_send()
+
+    def carries1(k):
+        return via1_here & among(RELAYED_LEFT, run, k)
+
+    def carries2(k):
+        return via2_here & among(RELAYED_RIGHT, run - 1, k)
+
+    def relay1(k):
+        @pl.when(carries1(k))
+        def _():
+            via_bulk1(k).wait_recv()
+            on_bulk1(k).start()
+            via_corner1(k).wait_recv()
+            on_corner1(k).start()
+
+    def relay2(k):
+        @pl.when(carries2(k))
+        def _():
+            via_corner2(k).wait_recv()
+            on_corner2(k).start()
+            via_bulk2(k).wait_recv()
+            on_bulk2(k).start()
 
     def fy2(k):
         return remote(fy2_s, fy2_r, fy2_ss, fy2_rs, k, {"fy": fy + 1})
@@ -249,10 +344,13 @@
             a, b = work[first + 2 * p, :, LANES:], work[first + 2 * p + 1, :, LANES:]
             fy1_s[k, p] = jnp.where(low_edge, roll(a, -border), roll(b, 64 - border))
         pl.when(has_up)(lambda: fy1(k).start())
+
+    def send_bulk(k):
+        first = k * GROUP
         pack_bulk(
             lambda c: work[first + c, :border, :LANES], lambda c: work[first + c, :border, LANES:], bulk1_s, k
         )
-        pl.when(has_left)(lambda: bulk1(k).start())
+        leftward(bulk1, via_bulk1, k, start)
 
     def send_columns(k):
         pl.when(has_down)(lambda: fy1(k).wait_recv())
@@ -262,7 +360,7 @@
             work[a, :, LANES:] = work[a, :, LANES:] + jnp.where(low_edge, strip, 0.0)
             work[a + 1, :, LANES:] = work[a + 1, :, LANES:] + jnp.where(low_edge, roll(strip, 64), 0.0)
         pack_corner(lambda c: work[k * GROUP + c, :border, LANES:], corner1_s, k)
-        pl.when(has_left)(lambda: corner1(k).start())
+        leftward(corner1, via_corner1, k, start)
 
     root = jnp.float32(0.5**0.5)
 
@@ -298,11 +396,11 @@
                 image_next[i, :, lanes] = step
                 work[i, border:, lanes] = (2.0 * step - image) * w
         pack_corner(lambda c: work[k * GROUP + c, tx:, LANES:], corner2_s, k)
-        pl.when(has_right)(lambda: corner2(k).start())
+        rightward(corner2, via_corner2, k, start)
         pack_bulk(
             lambda c: work[k * GROUP + c, tx:, :LANES], lambda c: work[k * GROUP + c, tx:, LANES:], bulk2_s, k
         )
-        pl.when(has_right)(lambda: bulk2(k).start())
+        rightward(bulk2, via_bulk2, k, start)
 
     def send_rows(k):
         pl.when(has_left)(lambda: corner2(k).wait_recv())
@@ -348,8 +446,21 @@
 
     for i in range(3):
         constant(i).wait()
-
-    phases = ((synthesize, 0), (send_columns, 1), (update_image, 3), (send_rows, 5), (analyse, 6))
+    for k in range(1, chunks):
+        load(dual_hbm, dual, dual_sem, k).start()
+    for k in range(chunks):
+        load(img_hbm, img, img_sem, k).start()
+        load(grad_hbm, grad, grad_sem, k).start()
+    for i in range(3, len(constants)):
+        constant(i).start()
+
+    image_lag, rows_lag = [jnp.where(crosses_right, *lags) for lags in (IMAGE_LAG, ROWS_LAG)]
+    phases = (
+        (synthesize, 0), (send_columns, 2), (send_bulk, 0), (relay1, RELAY_LAG[0]), (update_image, image_lag),
+        (relay2, RELAY_LAG[1]), (send_rows, rows_lag), (analyse, rows_lag + 1),
+    )
+    if not relays:
+        phases = tuple(p for p in phases if p[0] not in (relay1, relay2))
 
     def step(s, carry):
         for phase, lag in phases:
@@ -360,7 +471,7 @@
 
         return carry
 
-    lax.fori_loop(0, chunks + phases[-1][1], step, 0)
+    lax.fori_loop(0, chunks + rows_lag + 1, step, 0)
 
     swap = pltpu.make_async_remote_copy(
         src_ref=total, dst_ref=other, send_sem=ch_ss, recv_sem=ch_rs, device_id={"ch": 1 - ch}, device_id_type=MESH
@@ -370,15 +481,21 @@
     def drain(k, carry):
         pl.when(has_up)(lambda: fy1(k).wait_send())
 
-        @pl.when(has_left)
-        def _():
-            bulk1(k).wait_send()
-            corner1(k).wait_send()
-
-        @pl.when(has_right)
-        def _():
-            bulk2(k).wait_send()
-            corner2(k).wait_send()
+        leftward(bulk1, via_bulk1, k, wait_send)
+        leftward(corner1, via_corner1, k, wait_send)
+        rightward(corner2, via_corner2, k, wait_send)
+        rightward(bulk2, via_bulk2, k, wait_send)
+        if relays:
+
+            @pl.when(carries1(k))
+            def _():
+                on_bulk1(k).wait_send()
+                on_corner1(k).wait_send()
+
+            @pl.when(carries2(k))
+            def _():
+                on_bulk2(k).wait_send()
+                on_corner2(k).wait_send()
 
         pl.when(has_down)(lambda: fy2(k).wait_send())
         return carry
@@ -448,10 +565,10 @@
             pltpu.VMEM((GROUP * ex, ey + LANES), bf16),
             pltpu.VMEM((GROUP * ex, ey + LANES), bf16),
             pltpu.VMEM((GROUP * ex, ey + LANES), f32),
-            strip_y, strip_y, bulk, bulk, corner, corner, bulk, bulk, corner, corner, strip_y, strip_y,
+            strip_y, strip_y, bulk, bulk, corner, corner, bulk, bulk, corner, corner, strip_y, strip_y, bulk, corner,
             pltpu.VMEM((ex, ey), f32), pltpu.VMEM((ex, ey), f32),
             dma((chunks,)), dma((chunks,)), dma((chunks,)), dma((7,)),
-            *[dma((chunks,)) for _ in range(12)],
+            *[dma((chunks,)) for _ in range(16)],
             dma, dma,
         ],
         compiler_params=pltpu.CompilerParams(

time: 79.1 us -> 73.2 us (0.925)
  Pallas kernels: 78.2 us -> 72.5 us
    pallas_call x1, Pallas kernels: 75.6 us -> 69.9 us  [shards(): pl.pallas_call(functools.partial(kernel, sizes), out_shape=(jax.ShapeDtyp...]
where the time goes in v3:
time: 73.2 us; the launch traced here: 73.1 us
  Pallas kernels  72.5 us (99%)
    pallas_call x1, Pallas kernels, shards(): pl.pallas_call(functools.partial(kernel, sizes), out_shape=(jax.ShapeDtyp...  69.9 us
    pallas_call x1, Pallas kernels, shards(): pl.pallas_call(functools.partial(finish, chunks), out_shape=(jax.ShapeDty...  2.57 us

profile of v3, /device:TPU:22, one launch (start us, length us, event | category | flops | bytes accessed | tf_op | source)
XLA Modules:
  0.0 73.1 jit_solution(8282675868934904121)
XLA Ops:
  0.6 69.9 %primal_dual.1 = (f32[32,64,208]{2,1,0:T(8,128)S(1)}, f32[32,112,256]{2,1,0:T(8,128)S(1)}, f32[112,256]{1,0:T(8,128)S(1)}) custom-call(f32[32,64,208]{2,1,0:T(8,128)} %img_hbm.1, bf16[32,64,208]{2,1,0:T(8,128)(2,1)} %grad_hbm.1, f32[32,112,256]{2,1,0:T(8,128)} %dual_hbm.1, f32[112,256]{1,0:T(8,128)} %rw_hbm.1, bf16[2,224,112]{2,1,0:T(8,128)(2,1)} %constant.12.clone.lowx_hbm, ...), custom_call_target="tpu_custom_call" | custom-call | tf_op jit(solution)/shard_map/primal_dual/pallas_call | solution.py:549
  70.5 2.6 %scaled_results.1 = (f32[32,64,208]{2,1,0:T(8,128)}, f32[32,112,256]{2,1,0:T(8,128)}) custom-call(f32[32,64,208]{2,1,0:T(8,128)S(1)} %get-tuple-element.5.image, f32[32,112,256]{2,1,0:T(8,128)S(1)} %get-tuple-element.6.updated, f32[112,256]{1,0:T(8,128)S(1)} %get-tuple-element.7.factor), custom_call_target="tpu_custom_call" | custom-call | tf_op jit(solution)/shard_map/scaled_results/pallas_call | solution.py:579

commit v4 on v3

--- a/solution.py
+++ b/solution.py
@@ -273,6 +273,9 @@
     def fy2(k):
         return remote(fy2_s, fy2_r, fy2_ss, fy2_rs, k, {"fy": fy + 1})
 
+    def swap(side):
+        return remote(total, other, ch_ss, ch_rs, side, {"ch": 1 - ch})
+
     lane_e = lax.broadcasted_iota(jnp.int32, (ex, LANES), 1)
     lane_b = lax.broadcasted_iota(jnp.int32, (border, LANES), 1)
     lane_h = lax.broadcasted_iota(jnp.int32, (half, LANES), 1)
@@ -434,15 +437,16 @@
             lanes = slice(tile * LANES, (tile + 1) * LANES)
             return jnp.concatenate([mixed[c * ex : (c + 1) * ex, lanes] for c in range(GROUP)], axis=1)
 
-        low = dot3((lowxt[0], lowxt[1]), split(jnp.concatenate([beside(0), beside(1)], axis=0)))
-        high = dot3((wx[0], wx[1]), split(beside(2)))
-        for lanes, part in ((slice(0, LANES), low), (slice(LANES, 2 * LANES), high)):
-            squares = total[:, lanes]
+        for side, matrix, tiles in ((0, lowxt, (0, 1)), (1, wx, (2,))):
+            lanes = slice(side * LANES, (side + 1) * LANES)
+            part = dot3((matrix[0], matrix[1]), split(jnp.concatenate([beside(t) for t in tiles], axis=0)))
+            squares = total[side]
             for c in range(GROUP):
                 value = dual[first + c, :, lanes] + part[:, c * LANES : (c + 1) * LANES]
                 updated[first + c, :, lanes] = value
                 squares = squares + value * value
-            total[:, lanes] = squares
+            total[side] = squares
+            pl.when(k == chunks - 1)(lambda side=side: swap(side).start())
 
     for i in range(3):
         constant(i).wait()
@@ -473,11 +477,6 @@
 
     lax.fori_loop(0, chunks + rows_lag + 1, step, 0)
 
-    swap = pltpu.make_async_remote_copy(
-        src_ref=total, dst_ref=other, send_sem=ch_ss, recv_sem=ch_rs, device_id={"ch": 1 - ch}, device_id_type=MESH
-    )
-    swap.start()
-
     def drain(k, carry):
         pl.when(has_up)(lambda: fy1(k).wait_send())
 
@@ -501,28 +500,33 @@
         return carry
 
     lax.fori_loop(0, chunks, drain, 0)
-    swap.wait()
-    factor[...] = jnp.minimum(1.0, LAMBDA_REG * rw[...] / jnp.sqrt(total[...] + other[...] + EPSILON))
-
-
-def finish(chunks, image, updated, factor, image_out, dual_out, scaled, image_sem, sems):
-    pltpu.make_async_copy(image, image_out, image_sem).start()
-
-    def copy(k):
+    for side in range(2):
+        lanes = slice(side * LANES, (side + 1) * LANES)
+        swap(side).wait()
+        factor[:, lanes] = jnp.minimum(1.0, LAMBDA_REG * rw[:, lanes] * lax.rsqrt(total[side] + other[side] + EPSILON))
+
+
+def finish(chunks, image, updated, factor, image_out, dual_out, scaled, image_sems, sems):
+    def copies(k):
         rows = pl.ds(k * GROUP, GROUP)
-        return pltpu.make_async_copy(scaled.at[rows], dual_out.at[rows], sems.at[k])
+        return (
+            pltpu.make_async_copy(scaled.at[rows], dual_out.at[rows], sems.at[k]),
+            pltpu.make_async_copy(image.at[rows], image_out.at[rows], image_sems.at[k]),
+        )
 
     def step(k, carry):
+        dual_copy, image_copy = copies(k)
+        image_copy.start()
         for c in range(GROUP):
             scaled[k * GROUP + c] = updated[k * GROUP + c] * factor[...]
-        copy(k).start()
+        dual_copy.start()
         return carry
 
     lax.fori_loop(0, chunks, step, 0)
-    pltpu.make_async_copy(image, image_out, image_sem).wait()
 
     def drain(k, carry):
-        copy(k).wait()
+        for copy in copies(k):
+            copy.wait()
         return carry
 
     lax.fori_loop(0, chunks, drain, 0)
@@ -566,10 +570,10 @@
             pltpu.VMEM((GROUP * ex, ey + LANES), bf16),
             pltpu.VMEM((GROUP * ex, ey + LANES), f32),
             strip_y, strip_y, bulk, bulk, corner, corner, bulk, bulk, corner, corner, strip_y, strip_y, bulk, corner,
-            pltpu.VMEM((ex, ey), f32), pltpu.VMEM((ex, ey), f32),
+            pltpu.VMEM((2, ex, LANES), f32), pltpu.VMEM((2, ex, LANES), f32),
             dma((chunks,)), dma((chunks,)), dma((chunks,)), dma((7,)),
             *[dma((chunks,)) for _ in range(16)],
-            dma, dma,
+            dma((2,)), dma((2,)),
         ],
         compiler_params=pltpu.CompilerParams(
             collective_id=0, has_side_effects=True, vmem_limit_bytes=40 * 2**20
@@ -584,7 +588,7 @@
         ),
         in_specs=[in_vmem] * 3,
         out_specs=(in_hbm,) * 2,
-        scratch_shapes=[pltpu.VMEM(dual_coeffs.shape, f32), dma, dma((chunks,))],
+        scratch_shapes=[pltpu.VMEM(dual_coeffs.shape, f32), dma((chunks,)), dma((chunks,))],
         compiler_params=pltpu.CompilerParams(vmem_limit_bytes=16 * 2**20),
         name="scaled_results",
     )(image_next, updated, factor)

time: 73.2 us -> 73.5 us (level)
  no operation moved by 1% of the time
where the time goes in v4:
time: 73.5 us; the launch traced here: 73.2 us
  Pallas kernels  72.6 us (99%)
    pallas_call x1, Pallas kernels, shards(): pl.pallas_call(functools.partial(kernel, sizes), out_shape=(jax.ShapeDtyp...  69.9 us
    pallas_call x1, Pallas kernels, shards(): pl.pallas_call(functools.partial(finish, chunks), out_shape=(jax.ShapeDty...  2.63 us

profile of v4, /device:TPU:22, one launch (start us, length us, event | category | flops | bytes accessed | tf_op | source)
XLA Modules:
  0.0 73.2 jit_solution(14332248969168782872)
XLA Ops:
  0.6 69.9 %primal_dual.1 = (f32[32,64,208]{2,1,0:T(8,128)S(1)}, f32[32,112,256]{2,1,0:T(8,128)S(1)}, f32[112,256]{1,0:T(8,128)S(1)}) custom-call(f32[32,64,208]{2,1,0:T(8,128)} %img_hbm.1, bf16[32,64,208]{2,1,0:T(8,128)(2,1)} %grad_hbm.1, f32[32,112,256]{2,1,0:T(8,128)} %dual_hbm.1, f32[112,256]{1,0:T(8,128)} %rw_hbm.1, bf16[2,224,112]{2,1,0:T(8,128)(2,1)} %constant.12.clone.lowx_hbm, ...), custom_call_target="tpu_custom_call" | custom-call | tf_op jit(solution)/shard_map/primal_dual/pallas_call | solution.py:553
  70.6 2.6 %scaled_results.1 = (f32[32,64,208]{2,1,0:T(8,128)}, f32[32,112,256]{2,1,0:T(8,128)}) custom-call(f32[32,64,208]{2,1,0:T(8,128)S(1)} %get-tuple-element.5.image, f32[32,112,256]{2,1,0:T(8,128)S(1)} %get-tuple-element.6.updated, f32[112,256]{1,0:T(8,128)S(1)} %get-tuple-element.7.factor), custom_call_target="tpu_custom_call" | custom-call | tf_op jit(solution)/shard_map/scaled_results/pallas_call | solution.py:583

commit v5 on v3

--- a/solution.py
+++ b/solution.py
@@ -316,8 +316,14 @@
 
     def put_rows(at, lanes, value):
         high = value.astype(jnp.bfloat16)
-        rows_hi[at : at + ex, lanes] = high
-        rows_lo[at : at + ex, lanes] = (value - high.astype(jnp.float32)).astype(jnp.bfloat16)
+        rows = slice(at, at + value.shape[0])
+        rows_hi[rows, lanes] = high
+        rows_lo[rows, lanes] = (value - high.astype(jnp.float32)).astype(jnp.bfloat16)
+
+    def put_edge_first(c, tile, value):
+        lanes = slice(tile * LANES, (tile + 1) * LANES)
+        put_rows(c * border, lanes, value[:border])
+        put_rows(GROUP * border + c * tx, lanes, value[border:])
 
     def synthesize(k):
         load(dual_hbm, dual, dual_sem, k).wait()
@@ -326,20 +332,25 @@
         from_left = dot3((lowx[0], lowx[1]), split(left))
         for c in range(GROUP):
             lanes = slice(c * LANES, (c + 1) * LANES)
-            put_rows(c * ex, slice(0, LANES), from_left[:ex, lanes])
-            put_rows(c * ex, slice(LANES, 2 * LANES), from_left[ex:, lanes])
+            put_edge_first(c, 0, from_left[:ex, lanes])
+            put_edge_first(c, 1, from_left[ex:, lanes])
         right = jnp.concatenate([dual[first + c, :, LANES:] for c in range(GROUP)], axis=1)
         from_right = dot3((wxt[0], wxt[1]), split(right))
         for c in range(GROUP):
-            put_rows(c * ex, slice(2 * LANES, 3 * LANES), from_right[:, c * LANES : (c + 1) * LANES])
-        result = dot3((rows_hi[...], rows_lo[...]), (ay[0], ay[1]))
-        for c in range(GROUP):
-            work[first + c] = result[c * ex : (c + 1) * ex]
+            put_edge_first(c, 2, from_right[:, c * LANES : (c + 1) * LANES])
+        edges = GROUP * border
+        result = dot3((rows_hi[:edges], rows_lo[:edges]), (ay[0], ay[1]))
+        for c in range(GROUP):
+            work[first + c, :border] = result[c * border : (c + 1) * border]
 
         @pl.when(k == 0)
         def _():
             pl.semaphore_wait(barrier, neighbours)
-
+            send_bulk(k)
+
+        result = dot3((rows_hi[edges:], rows_lo[edges:]), (ay[0], ay[1]))
+        for c in range(GROUP):
+            work[first + c, border:] = result[c * tx : (c + 1) * tx]
         for p in range(GROUP // 2):
             a, b = work[first + 2 * p, :, LANES:], work[first + 2 * p + 1, :, LANES:]
             fy1_s[k, p] = jnp.where(low_edge, roll(a, -border), roll(b, 64 - border))
@@ -351,6 +362,9 @@
             lambda c: work[first + c, :border, :LANES], lambda c: work[first + c, :border, LANES:], bulk1_s, k
         )
         leftward(bulk1, via_bulk1, k, start)
+
+    def send_later_bulk(k):
+        pl.when(k > 0)(lambda: send_bulk(k))
 
     def send_columns(k):
         pl.when(has_down)(lambda: fy1(k).wait_recv())
@@ -456,7 +470,7 @@
 
     image_lag, rows_lag = [jnp.where(crosses_right, *lags) for lags in (IMAGE_LAG, ROWS_LAG)]
     phases = (
-        (synthesize, 0), (send_columns, 2), (send_bulk, 0), (relay1, RELAY_LAG[0]), (update_image, image_lag),
+        (synthesize, 0), (send_columns, 2), (send_later_bulk, 0), (relay1, RELAY_LAG[0]), (update_image, image_lag),
         (relay2, RELAY_LAG[1]), (send_rows, rows_lag), (analyse, rows_lag + 1),
     )
     if not relays:

time: 73.2 us -> 74.9 us (1.023)
  the two profiles are of different devices: /device:TPU:22 before, /device:TPU:42 now
where the time goes in v5:
time: 74.9 us; the launch traced here: 74.8 us
  Pallas kernels  74.1 us (99%)
    pallas_call x1, Pallas kernels, shards(): pl.pallas_call(functools.partial(kernel, sizes), out_shape=(jax.ShapeDtyp...  71.6 us
    pallas_call x1, Pallas kernels, shards(): pl.pallas_call(functools.partial(finish, chunks), out_shape=(jax.ShapeDty...  2.57 us

profile of v5, /device:TPU:42, one launch (start us, length us, event | category | flops | bytes accessed | tf_op | source)
XLA Modules:
  0.0 74.8 jit_solution(7026208328563936854)
XLA Ops:
  0.6 71.6 %primal_dual.1 = (f32[32,64,208]{2,1,0:T(8,128)S(1)}, f32[32,112,256]{2,1,0:T(8,128)S(1)}, f32[112,256]{1,0:T(8,128)S(1)}) custom-call(f32[32,64,208]{2,1,0:T(8,128)} %img_hbm.1, bf16[32,64,208]{2,1,0:T(8,128)(2,1)} %grad_hbm.1, f32[32,112,256]{2,1,0:T(8,128)} %dual_hbm.1, f32[112,256]{1,0:T(8,128)} %rw_hbm.1, bf16[2,224,112]{2,1,0:T(8,128)(2,1)} %constant.12.clone.lowx_hbm, ...), custom_call_target="tpu_custom_call" | custom-call | tf_op jit(solution)/shard_map/primal_dual/pallas_call | solution.py:563
  72.2 2.6 %scaled_results.1 = (f32[32,64,208]{2,1,0:T(8,128)}, f32[32,112,256]{2,1,0:T(8,128)}) custom-call(f32[32,64,208]{2,1,0:T(8,128)S(1)} %get-tuple-element.5.image, f32[32,112,256]{2,1,0:T(8,128)S(1)} %get-tuple-element.6.updated, f32[112,256]{1,0:T(8,128)S(1)} %get-tuple-element.7.factor), custom_call_target="tpu_custom_call" | custom-call | tf_op jit(solution)/shard_map/scaled_results/pallas_call | solution.py:593
